TPU v7x, 32 devices: a whole 2x2x4 slice. The times are simulated.
32 devices in a mesh: py: 2 (over core), px: 2 (over y), pz: 2 (over x), site: 4 (over z).
Axes of the slice: x: 2, y: 2, z: 4, core: 2. Of those that a mesh axis runs over, the one named last changes fastest.
Arguments:
- density: float32 [256, 8, 128, 128], P(('site', 'py'), 'px', 'pz'), parts along dimension 0, may hold values from 0.2 to 1.8
- diffusivity: float32 [256, 8, 128, 128], P(('site', 'py'), 'px', 'pz'), parts along dimension 0, may hold values from 0.03 to 0.15
- source: float32 [256, 8, 128, 128], P(('site', 'py'), 'px', 'pz'), parts along dimension 0, may hold values from -0.2 to 0.2
Outputs:
- density_end: float32 [256, 8, 128, 128], P(('site', 'py'), 'px', 'pz'), parts along dimension 0
There are 4 independent parts, one for each index of `site`. A program takes and returns all parts, laid end to end along the dimension named above; each array names one. Nothing has to cross between parts.
All inputs are finite; a program needn't handle non-finite values.
Results may differ from a plain program's by a relative error of at most 0.00002.
Values sent between devices are 32-bit elements; how exact they have to be, the bound alone decides.
A program may use at most 192 MiB of HBM per device.

v0:
```python
import jax
import jax.numpy as jnp
from jax import lax
from jax.sharding import PartitionSpec as P

STEPS = 4


def padded_2(cells, sides, width):
    for axis, dim in sides:
        count = lax.axis_size(axis)
        ends = count - 1
        head = lax.slice_in_dim(cells, 0, width, axis=dim)
        tail = lax.slice_in_dim(cells, cells.shape[dim] - width, cells.shape[dim], axis=dim)
        cells = jnp.concatenate(
            [
                lax.ppermute(tail, axis, [(i, (i + 1) % count) for i in range(ends)]),
                cells,
                lax.ppermute(head, axis, [((i + 1) % count, i) for i in range(ends)]),
            ],
            axis=dim,
        )
    return cells


def inner_cells(values, dims):
    for dim in dims:
        values = lax.slice_in_dim(values, 1, values.shape[dim] - 1, axis=dim)
    return values


def side_cells(values, dim, start, dims):
    others = [other for other in dims if other != dim]
    values = inner_cells(values, others)
    return lax.slice_in_dim(values, start, start + values.shape[dim] - 2, axis=dim)


def advance(padded, diffusivity, source):
    middle = inner_cells(padded, (0, 1, 2))
    lower = [side_cells(padded, dim, 0, (0, 1, 2)) for dim in (0, 1, 2)]
    upper = [side_cells(padded, dim, 2, (0, 1, 2)) for dim in (0, 1, 2)]
    spread = lower[0] + upper[0] + lower[1] + upper[1] + lower[2] + upper[2] - 6.0 * middle
    return middle + diffusivity * spread + source


def body(density, diffusivity, source):
    for step in range(STEPS):
        padded = padded_2(density, (("py", 0), ("px", 1), ("pz", 2)), 1)
        density = advance(padded, diffusivity, source)
    return density


def solution(mesh):
    placed = (
        P(("site", "py"), "px", "pz", None),
        P(("site", "py"), "px", "pz", None),
        P(("site", "py"), "px", "pz", None),
    )
    return jax.shard_map(
        body,
        mesh=mesh,
        in_specs=placed,
        out_specs=P(("site", "py"), "px", "pz", None),
        check_vma=False,
    )
```

profile of v0, /device:TPU:0, one launch (start us, length us, event | category | flops | bytes accessed | tf_op | source)
XLA Modules:
  0.0 246.4 jit_solution(2932186284840022996)
XLA Ops:
  1.0 2.4 collective-permute-start
  4.7 2.5 %constant_dynamic-update-slice_fusion.1 = f32[34,4,64,128]{3,2,1,0:T(8,128)S(1)} fusion(f32[34,4,64,128]{3,2,1,0:T(8,128)S(1)} %constant_dynamic-update-slice_fusion.2, f32[32,4,64,128]{3,2,1,0:T(8,128)} %param.3), kind=kLoop, calls=%fused_computation.128 | loop fusion | bytes 8388608
  7.5 4.3 %collective-permute-start.2 = (f32[34,1,64,128]{3,2,1,0:T(8,128)S(1)}, f32[34,1,64,128]{3,2,1,0:T(8,128)S(1)}, u32[]{:S(2)}, u32[]{:S(2)}) collective-permute-start(f32[34,1,64,128]{3,2,1,0:T(8,128)S(1)} %get-tuple-element.19), channel_id=1, source_target_pairs={{0,8},{1,9},{2,10},{3,11},{4,12},{5,13},{6,14},{7,15},{16,24},{17,... | collective-permute-start | bytes 3342344 | tf_op jit(solution)/shard_map/ppermute | solution.py:17
  11.9 1.3 collective-permute-start.3
  13.2 23.4 %collective-permute-done.2 = f32[34,1,64,128]{3,2,1,0:T(8,128)S(1)} collective-permute-done((f32[34,1,64,128]{3,2,1,0:T(8,128)S(1)}, f32[34,1,64,128]{3,2,1,0:T(8,128)S(1)}, u32[]{:S(2)}, u32[]{:S(2)}) %collective-permute-start.2) | collective-permute-done | bytes 1114144 | tf_op jit(solution)/shard_map/ppermute | solution.py:17
  36.6 4.5 %collective-permute-done.3 = f32[34,1,64,128]{3,2,1,0:T(8,128)S(1)} collective-permute-done((f32[34,1,64,128]{3,2,1,0:T(8,128)S(1)}, f32[34,1,64,128]{3,2,1,0:T(8,128)S(1)}, u32[]{:S(2)}, u32[]{:S(2)}) %collective-permute-start.3) | collective-permute-done | bytes 1114144 | tf_op jit(solution)/shard_map/ppermute | solution.py:19
  42.6 4.6 %collective-permute-start.4 = (f32[34,6,1,128]{3,0,2,1:T(8,128)S(1)}, f32[34,6,1,128]{3,0,2,1:T(8,128)S(1)}, u32[]{:S(2)}, u32[]{:S(2)}) collective-permute-start(f32[34,6,1,128]{3,0,2,1:T(8,128)S(1)} %copy.20), channel_id=1, source_target_pairs={{0,4},{1,5},{2,6},{3,7},{8,12},{9,13},{10,14},{11,15},{16,20},{17,... | collective-permute-start | bytes 313352 | tf_op jit(solution)/shard_map/ppermute | solution.py:17
  49.7 19.2 %fusion.31 = f32[32,4,64,128]{3,2,1,0:T(8,128)S(1)} fusion(f32[32,4,64,128]{3,2,1,0:T(8,128)} %param.5, f32[32,4,64,128]{3,2,1,0:T(8,128)} %param.3, f32[32,4,64,128]{3,2,1,0:T(8,128)} %param.4, f32[34,6,1,128]{3,2,1,0:T(1,128)S(1)} %copy.23, f32[34,1,64,128]{3,2,1,0:T(8,128)S(1)} %collective-permute-done.3, f32[34,4,64,128]{3,2,1,0:T(8,128)} %copy-done.2, ...), kind=kLoop, calls=%fused_computation.86 | loop fusion | flops 20971520 | bytes 23932928 | tf_op jit(solution)/shard_map/add | solution.py:43
  68.9 1.3 collective-permute-start.6
  70.2 1.3 collective-permute-start.7
  71.5 1.9 collective-permute-done.7
  73.7 1.5 collective-permute-start.8
  76.6 22.9 %collective-permute-done.8 = f32[34,1,64,128]{3,2,1,0:T(8,128)S(1)} collective-permute-done((f32[34,1,64,128]{3,2,1,0:T(8,128)S(1)}, f32[34,1,64,128]{3,2,1,0:T(8,128)S(1)}, u32[]{:S(2)}, u32[]{:S(2)}) %collective-permute-start.8) | collective-permute-done | bytes 1114144 | tf_op jit(solution)/shard_map/ppermute | solution.py:17
  99.4 4.2 %collective-permute-done.9 = f32[34,1,64,128]{3,2,1,0:T(8,128)S(1)} collective-permute-done((f32[34,1,64,128]{3,2,1,0:T(8,128)S(1)}, f32[34,1,64,128]{3,2,1,0:T(8,128)S(1)}, u32[]{:S(2)}, u32[]{:S(2)}) %collective-permute-start.9) | collective-permute-done | bytes 1114144 | tf_op jit(solution)/shard_map/ppermute | solution.py:19
  103.8 1.3 collective-permute-start.11
  105.1 4.6 %collective-permute-start.10 = (f32[34,6,1,128]{3,0,2,1:T(8,128)S(1)}, f32[34,6,1,128]{3,0,2,1:T(8,128)S(1)}, u32[]{:S(2)}, u32[]{:S(2)}) collective-permute-start(f32[34,6,1,128]{3,0,2,1:T(8,128)S(1)} %copy.24), channel_id=1, source_target_pairs={{0,4},{1,5},{2,6},{3,7},{8,12},{9,13},{10,14},{11,15},{16,20},{17,... | collective-permute-start | bytes 313352 | tf_op jit(solution)/shard_map/ppermute | solution.py:17
  112.8 20.0 %fusion.22 = f32[32,4,64,128]{3,2,1,0:T(8,128)S(1)} fusion(f32[32,4,64,128]{3,2,1,0:T(8,128)} %param.5, f32[32,4,64,128]{3,2,1,0:T(8,128)} %copy-done.1, f32[32,4,64,128]{3,2,1,0:T(8,128)} %param.4, f32[34,6,1,128]{3,2,1,0:T(1,128)} %copy.27, f32[34,1,64,128]{3,2,1,0:T(8,128)S(1)} %collective-permute-done.9, ...), kind=kLoop, calls=%fused_computation.59 | loop fusion | flops 29360128 | bytes 19476480 | tf_op jit(solution)/shard_map/add | solution.py:43
  132.9 1.3 collective-permute-start.12
  135.5 1.9 collective-permute-done.13
  137.6 1.5 collective-permute-start.14
  140.5 22.9 %collective-permute-done.14 = f32[34,1,64,128]{3,2,1,0:T(8,128)S(1)} collective-permute-done((f32[34,1,64,128]{3,2,1,0:T(8,128)S(1)}, f32[34,1,64,128]{3,2,1,0:T(8,128)S(1)}, u32[]{:S(2)}, u32[]{:S(2)}) %collective-permute-start.14) | collective-permute-done | bytes 1114144 | tf_op jit(solution)/shard_map/ppermute | solution.py:17
  163.3 4.2 %collective-permute-done.15 = f32[34,1,64,128]{3,2,1,0:T(8,128)S(1)} collective-permute-done((f32[34,1,64,128]{3,2,1,0:T(8,128)S(1)}, f32[34,1,64,128]{3,2,1,0:T(8,128)S(1)}, u32[]{:S(2)}, u32[]{:S(2)}) %collective-permute-start.15) | collective-permute-done | bytes 1114144 | tf_op jit(solution)/shard_map/ppermute | solution.py:19
  169.0 4.7 %collective-permute-start.16 = (f32[34,6,1,128]{3,0,2,1:T(8,128)S(1)}, f32[34,6,1,128]{3,0,2,1:T(8,128)S(1)}, u32[]{:S(2)}, u32[]{:S(2)}) collective-permute-start(f32[34,6,1,128]{3,0,2,1:T(8,128)S(1)} %copy.28), channel_id=1, source_target_pairs={{0,4},{1,5},{2,6},{3,7},{8,12},{9,13},{10,14},{11,15},{16,20},{17,... | collective-permute-start | bytes 313352 | tf_op jit(solution)/shard_map/ppermute | solution.py:17
  176.7 11.5 %fusion.13 = f32[32,4,64,128]{3,2,1,0:T(8,128)} fusion(f32[32,4,64,128]{3,2,1,0:T(8,128)} %param.5, f32[32,4,64,128]{3,2,1,0:T(8,128)S(1)} %fusion.22, f32[32,4,64,128]{3,2,1,0:T(8,128)} %param.4, f32[34,6,1,128]{3,2,1,0:T(1,128)} %copy.31, f32[34,1,64,128]{3,2,1,0:T(8,128)S(1)} %collective-permute-done.15, ...), kind=kLoop, calls=%fused_computation.32 | loop fusion | flops 29360128 | bytes 19476480 | tf_op jit(solution)/shard_map/add | solution.py:43
  189.4 1.4 collective-permute-start.18
  192.1 1.9 collective-permute-done.19
  194.1 1.7 pad_maximum_fusion.66
  195.8 1.5 collective-permute-start.20
  198.6 22.9 %collective-permute-done.20 = f32[34,1,64,128]{3,2,1,0:T(8,128)S(1)} collective-permute-done((f32[34,1,64,128]{3,2,1,0:T(8,128)S(1)}, f32[34,1,64,128]{3,2,1,0:T(8,128)S(1)}, u32[]{:S(2)}, u32[]{:S(2)}) %collective-permute-start.20) | collective-permute-done | bytes 1114144 | tf_op jit(solution)/shard_map/ppermute | solution.py:17
  221.4 4.2 %collective-permute-done.21 = f32[34,1,64,128]{3,2,1,0:T(8,128)S(1)} collective-permute-done((f32[34,1,64,128]{3,2,1,0:T(8,128)S(1)}, f32[34,1,64,128]{3,2,1,0:T(8,128)S(1)}, u32[]{:S(2)}, u32[]{:S(2)}) %collective-permute-start.21) | collective-permute-done | bytes 1114144 | tf_op jit(solution)/shard_map/ppermute | solution.py:19
  227.1 4.6 %collective-permute-start.22 = (f32[34,6,1,128]{3,0,2,1:T(8,128)S(1)}, f32[34,6,1,128]{3,0,2,1:T(8,128)S(1)}, u32[]{:S(2)}, u32[]{:S(2)}) collective-permute-start(f32[34,6,1,128]{3,0,2,1:T(8,128)S(1)} %copy.32), channel_id=1, source_target_pairs={{0,4},{1,5},{2,6},{3,7},{8,12},{9,13},{10,14},{11,15},{16,20},{17,... | collective-permute-start | bytes 313352 | tf_op jit(solution)/shard_map/ppermute | solution.py:17
  234.9 11.5 %fusion.4 = f32[32,4,64,128]{3,2,1,0:T(8,128)} fusion(f32[32,4,64,128]{3,2,1,0:T(8,128)} %param.5, f32[32,4,64,128]{3,2,1,0:T(8,128)S(1)} %copy-done, f32[32,4,64,128]{3,2,1,0:T(8,128)} %param.4, f32[34,6,1,128]{3,2,1,0:T(1,128)} %copy.35, f32[34,1,64,128]{3,2,1,0:T(8,128)S(1)} %collective-permute-done.21, f32[34,1,64,128]{3,2,1,0:T(8,128)S(1)} %collective-permute-done.20, ...), kind=kLoop, calls=%fused_computation.5 | loop fusion | flops 29360128 | bytes 19476480 | tf_op jit(solution)/shard_map/add | solution.py:43
  (57 shorter events, 27.0 us)
Async XLA Ops:
  1.0 3.7 %collective-permute-start = (f32[1,4,64,128]{3,2,1,0:T(8,128)S(1)}, f32[1,4,64,128]{3,2,1,0:T(8,128)S(1)}, u32[]{:S(2)}, u32[]{:S(2)}) collective-permute-start(f32[1,4,64,128]{3,2,1,0:T(8,128)S(1)} %get-tuple-element.28), channel_id=1, source_target_pairs={{0,16},{1,17},{2,18},{3,19},{4,20},{5,21},{6,22},{7,23},{8,24},{9,... | collective-permute-start | bytes 393224 | tf_op jit(solution)/shard_map/ppermute | solution.py:17
  3.4 3.8 %collective-permute-start.1 = (f32[1,4,64,128]{3,2,1,0:T(8,128)S(1)}, f32[1,4,64,128]{3,2,1,0:T(8,128)S(1)}, u32[]{:S(2)}, u32[]{:S(2)}) collective-permute-start(f32[1,4,64,128]{3,2,1,0:T(8,128)S(1)} %get-tuple-element.27), channel_id=1, source_target_pairs={{16,0},{17,1},{18,2},{19,3},{20,4},{21,5},{22,6},{23,7},{24,8},{25... | collective-permute-start | bytes 393224 | tf_op jit(solution)/shard_map/ppermute | solution.py:19
  7.3 34.0 %copy-start.2 = (f32[34,4,64,128]{3,2,1,0:T(8,128)}, f32[34,4,64,128]{3,2,1,0:T(8,128)S(1)}, u32[]{:S(2)}) copy-start(f32[34,4,64,128]{3,2,1,0:T(8,128)S(1)} %constant_dynamic-update-slice_fusion) | copy-start | bytes 13369348
  7.5 29.0 %collective-permute-start.2 = (f32[34,1,64,128]{3,2,1,0:T(8,128)S(1)}, f32[34,1,64,128]{3,2,1,0:T(8,128)S(1)}, u32[]{:S(2)}, u32[]{:S(2)}) collective-permute-start(f32[34,1,64,128]{3,2,1,0:T(8,128)S(1)} %get-tuple-element.19), channel_id=1, source_target_pairs={{0,8},{1,9},{2,10},{3,11},{4,12},{5,13},{6,14},{7,15},{16,24},{17,... | collective-permute-start | bytes 3342344 | tf_op jit(solution)/shard_map/ppermute | solution.py:17
  11.9 29.2 %collective-permute-start.3 = (f32[34,1,64,128]{3,2,1,0:T(8,128)S(1)}, f32[34,1,64,128]{3,2,1,0:T(8,128)S(1)}, u32[]{:S(2)}, u32[]{:S(2)}) collective-permute-start(f32[34,1,64,128]{3,2,1,0:T(8,128)S(1)} %get-tuple-element.20), channel_id=1, source_target_pairs={{8,0},{9,1},{10,2},{11,3},{12,4},{13,5},{14,6},{15,7},{24,16},{25,... | collective-permute-start | bytes 3342344 | tf_op jit(solution)/shard_map/ppermute | solution.py:19
  41.2 7.1 %collective-permute-start.5 = (f32[34,6,1,128]{3,0,2,1:T(8,128)S(1)}, f32[34,6,1,128]{3,0,2,1:T(8,128)S(1)}, u32[]{:S(2)}, u32[]{:S(2)}) collective-permute-start(f32[34,6,1,128]{3,0,2,1:T(8,128)S(1)} %copy.22), channel_id=1, source_target_pairs={{4,0},{5,1},{6,2},{7,3},{12,8},{13,9},{14,10},{15,11},{20,16},{21,... | collective-permute-start | bytes 313352 | tf_op jit(solution)/shard_map/ppermute | solution.py:19
  42.6 7.0 %collective-permute-start.4 = (f32[34,6,1,128]{3,0,2,1:T(8,128)S(1)}, f32[34,6,1,128]{3,0,2,1:T(8,128)S(1)}, u32[]{:S(2)}, u32[]{:S(2)}) collective-permute-start(f32[34,6,1,128]{3,0,2,1:T(8,128)S(1)} %copy.20), channel_id=1, source_target_pairs={{0,4},{1,5},{2,6},{3,7},{8,12},{9,13},{10,14},{11,15},{16,20},{17,... | collective-permute-start | bytes 313352 | tf_op jit(solution)/shard_map/ppermute | solution.py:17
  68.9 34.9 %copy-start.1 = (f32[32,4,64,128]{3,2,1,0:T(8,128)}, f32[32,4,64,128]{3,2,1,0:T(8,128)S(1)}, u32[]{:S(2)}) copy-start(f32[32,4,64,128]{3,2,1,0:T(8,128)S(1)} %fusion.31) | copy-start | bytes 12582916
  68.9 2.6 %collective-permute-start.6 = (f32[1,4,64,128]{3,2,1,0:T(8,128)S(1)}, f32[1,4,64,128]{3,2,1,0:T(8,128)S(1)}, u32[]{:S(2)}, u32[]{:S(2)}) collective-permute-start(f32[1,4,64,128]{3,2,1,0:T(8,128)S(1)} %get-tuple-element.25), channel_id=1, source_target_pairs={{0,16},{1,17},{2,18},{3,19},{4,20},{5,21},{6,22},{7,23},{8,24},{9,... | collective-permute-start | bytes 393224 | tf_op jit(solution)/shard_map/ppermute | solution.py:17
  70.2 3.2 %collective-permute-start.7 = (f32[1,4,64,128]{3,2,1,0:T(8,128)S(1)}, f32[1,4,64,128]{3,2,1,0:T(8,128)S(1)}, u32[]{:S(2)}, u32[]{:S(2)}) collective-permute-start(f32[1,4,64,128]{3,2,1,0:T(8,128)S(1)} %get-tuple-element.26), channel_id=1, source_target_pairs={{16,0},{17,1},{18,2},{19,3},{20,4},{21,5},{22,6},{23,7},{24,8},{25... | collective-permute-start | bytes 393224 | tf_op jit(solution)/shard_map/ppermute | solution.py:19
  73.7 25.7 %collective-permute-start.8 = (f32[34,1,64,128]{3,2,1,0:T(8,128)S(1)}, f32[34,1,64,128]{3,2,1,0:T(8,128)S(1)}, u32[]{:S(2)}, u32[]{:S(2)}) collective-permute-start(f32[34,1,64,128]{3,2,1,0:T(8,128)S(1)} %get-tuple-element.17), channel_id=1, source_target_pairs={{0,8},{1,9},{2,10},{3,11},{4,12},{5,13},{6,14},{7,15},{16,24},{17,... | collective-permute-start | bytes 3342344 | tf_op jit(solution)/shard_map/ppermute | solution.py:17
  75.3 28.4 %collective-permute-start.9 = (f32[34,1,64,128]{3,2,1,0:T(8,128)S(1)}, f32[34,1,64,128]{3,2,1,0:T(8,128)S(1)}, u32[]{:S(2)}, u32[]{:S(2)}) collective-permute-start(f32[34,1,64,128]{3,2,1,0:T(8,128)S(1)} %get-tuple-element.18), channel_id=1, source_target_pairs={{8,0},{9,1},{10,2},{11,3},{12,4},{13,5},{14,6},{15,7},{24,16},{25,... | collective-permute-start | bytes 3342344 | tf_op jit(solution)/shard_map/ppermute | solution.py:19
  103.8 6.8 %collective-permute-start.11 = (f32[34,6,1,128]{3,0,2,1:T(8,128)S(1)}, f32[34,6,1,128]{3,0,2,1:T(8,128)S(1)}, u32[]{:S(2)}, u32[]{:S(2)}) collective-permute-start(f32[34,6,1,128]{3,0,2,1:T(8,128)S(1)} %copy.26), channel_id=1, source_target_pairs={{4,0},{5,1},{6,2},{7,3},{12,8},{13,9},{14,10},{15,11},{20,16},{21,... | collective-permute-start | bytes 313352 | tf_op jit(solution)/shard_map/ppermute | solution.py:19
  105.1 7.0 %collective-permute-start.10 = (f32[34,6,1,128]{3,0,2,1:T(8,128)S(1)}, f32[34,6,1,128]{3,0,2,1:T(8,128)S(1)}, u32[]{:S(2)}, u32[]{:S(2)}) collective-permute-start(f32[34,6,1,128]{3,0,2,1:T(8,128)S(1)} %copy.24), channel_id=1, source_target_pairs={{0,4},{1,5},{2,6},{3,7},{8,12},{9,13},{10,14},{11,15},{16,20},{17,... | collective-permute-start | bytes 313352 | tf_op jit(solution)/shard_map/ppermute | solution.py:17
  132.9 2.6 %collective-permute-start.12 = (f32[1,4,64,128]{3,2,1,0:T(8,128)S(1)}, f32[1,4,64,128]{3,2,1,0:T(8,128)S(1)}, u32[]{:S(2)}, u32[]{:S(2)}) collective-permute-start(f32[1,4,64,128]{3,2,1,0:T(8,128)S(1)} %get-tuple-element.23), channel_id=1, source_target_pairs={{0,16},{1,17},{2,18},{3,19},{4,20},{5,21},{6,22},{7,23},{8,24},{9,... | collective-permute-start | bytes 393224 | tf_op jit(solution)/shard_map/ppermute | solution.py:17
  134.2 3.2 %collective-permute-start.13 = (f32[1,4,64,128]{3,2,1,0:T(8,128)S(1)}, f32[1,4,64,128]{3,2,1,0:T(8,128)S(1)}, u32[]{:S(2)}, u32[]{:S(2)}) collective-permute-start(f32[1,4,64,128]{3,2,1,0:T(8,128)S(1)} %get-tuple-element.24), channel_id=1, source_target_pairs={{16,0},{17,1},{18,2},{19,3},{20,4},{21,5},{22,6},{23,7},{24,8},{25... | collective-permute-start | bytes 393224 | tf_op jit(solution)/shard_map/ppermute | solution.py:19
  137.6 25.7 %collective-permute-start.14 = (f32[34,1,64,128]{3,2,1,0:T(8,128)S(1)}, f32[34,1,64,128]{3,2,1,0:T(8,128)S(1)}, u32[]{:S(2)}, u32[]{:S(2)}) collective-permute-start(f32[34,1,64,128]{3,2,1,0:T(8,128)S(1)} %get-tuple-element.15), channel_id=1, source_target_pairs={{0,8},{1,9},{2,10},{3,11},{4,12},{5,13},{6,14},{7,15},{16,24},{17,... | collective-permute-start | bytes 3342344 | tf_op jit(solution)/shard_map/ppermute | solution.py:17
  139.2 28.4 %collective-permute-start.15 = (f32[34,1,64,128]{3,2,1,0:T(8,128)S(1)}, f32[34,1,64,128]{3,2,1,0:T(8,128)S(1)}, u32[]{:S(2)}, u32[]{:S(2)}) collective-permute-start(f32[34,1,64,128]{3,2,1,0:T(8,128)S(1)} %get-tuple-element.16), channel_id=1, source_target_pairs={{8,0},{9,1},{10,2},{11,3},{12,4},{13,5},{14,6},{15,7},{24,16},{25,... | collective-permute-start | bytes 3342344 | tf_op jit(solution)/shard_map/ppermute | solution.py:19
  167.7 6.8 %collective-permute-start.17 = (f32[34,6,1,128]{3,0,2,1:T(8,128)S(1)}, f32[34,6,1,128]{3,0,2,1:T(8,128)S(1)}, u32[]{:S(2)}, u32[]{:S(2)}) collective-permute-start(f32[34,6,1,128]{3,0,2,1:T(8,128)S(1)} %copy.30), channel_id=1, source_target_pairs={{4,0},{5,1},{6,2},{7,3},{12,8},{13,9},{14,10},{15,11},{20,16},{21,... | collective-permute-start | bytes 313352 | tf_op jit(solution)/shard_map/ppermute | solution.py:19
  169.0 7.0 %collective-permute-start.16 = (f32[34,6,1,128]{3,0,2,1:T(8,128)S(1)}, f32[34,6,1,128]{3,0,2,1:T(8,128)S(1)}, u32[]{:S(2)}, u32[]{:S(2)}) collective-permute-start(f32[34,6,1,128]{3,0,2,1:T(8,128)S(1)} %copy.28), channel_id=1, source_target_pairs={{0,4},{1,5},{2,6},{3,7},{8,12},{9,13},{10,14},{11,15},{16,20},{17,... | collective-permute-start | bytes 313352 | tf_op jit(solution)/shard_map/ppermute | solution.py:17
  188.2 37.4 %copy-start = (f32[32,4,64,128]{3,2,1,0:T(8,128)S(1)}, f32[32,4,64,128]{3,2,1,0:T(8,128)}, u32[]{:S(2)}) copy-start(f32[32,4,64,128]{3,2,1,0:T(8,128)} %fusion.13) | copy-start | bytes 12582916
  189.4 2.7 %collective-permute-start.18 = (f32[1,4,64,128]{3,2,1,0:T(8,128)S(1)}, f32[1,4,64,128]{3,2,1,0:T(8,128)S(1)}, u32[]{:S(2)}, u32[]{:S(2)}) collective-permute-start(f32[1,4,64,128]{3,2,1,0:T(8,128)S(1)} %get-tuple-element.21), channel_id=1, source_target_pairs={{0,16},{1,17},{2,18},{3,19},{4,20},{5,21},{6,22},{7,23},{8,24},{9,... | collective-permute-start | bytes 393224 | tf_op jit(solution)/shard_map/ppermute | solution.py:17
  190.8 3.2 %collective-permute-start.19 = (f32[1,4,64,128]{3,2,1,0:T(8,128)S(1)}, f32[1,4,64,128]{3,2,1,0:T(8,128)S(1)}, u32[]{:S(2)}, u32[]{:S(2)}) collective-permute-start(f32[1,4,64,128]{3,2,1,0:T(8,128)S(1)} %get-tuple-element.22), channel_id=1, source_target_pairs={{16,0},{17,1},{18,2},{19,3},{20,4},{21,5},{22,6},{23,7},{24,8},{25... | collective-permute-start | bytes 393224 | tf_op jit(solution)/shard_map/ppermute | solution.py:19
  195.8 25.7 %collective-permute-start.20 = (f32[34,1,64,128]{3,2,1,0:T(8,128)S(1)}, f32[34,1,64,128]{3,2,1,0:T(8,128)S(1)}, u32[]{:S(2)}, u32[]{:S(2)}) collective-permute-start(f32[34,1,64,128]{3,2,1,0:T(8,128)S(1)} %get-tuple-element.13), channel_id=1, source_target_pairs={{0,8},{1,9},{2,10},{3,11},{4,12},{5,13},{6,14},{7,15},{16,24},{17,... | collective-permute-start | bytes 3342344 | tf_op jit(solution)/shard_map/ppermute | solution.py:17
  197.3 28.4 %collective-permute-start.21 = (f32[34,1,64,128]{3,2,1,0:T(8,128)S(1)}, f32[34,1,64,128]{3,2,1,0:T(8,128)S(1)}, u32[]{:S(2)}, u32[]{:S(2)}) collective-permute-start(f32[34,1,64,128]{3,2,1,0:T(8,128)S(1)} %get-tuple-element.14), channel_id=1, source_target_pairs={{8,0},{9,1},{10,2},{11,3},{12,4},{13,5},{14,6},{15,7},{24,16},{25,... | collective-permute-start | bytes 3342344 | tf_op jit(solution)/shard_map/ppermute | solution.py:19
  225.8 6.8 %collective-permute-start.23 = (f32[34,6,1,128]{3,0,2,1:T(8,128)S(1)}, f32[34,6,1,128]{3,0,2,1:T(8,128)S(1)}, u32[]{:S(2)}, u32[]{:S(2)}) collective-permute-start(f32[34,6,1,128]{3,0,2,1:T(8,128)S(1)} %copy.34), channel_id=1, source_target_pairs={{4,0},{5,1},{6,2},{7,3},{12,8},{13,9},{14,10},{15,11},{20,16},{21,... | collective-permute-start | bytes 313352 | tf_op jit(solution)/shard_map/ppermute | solution.py:19
  227.1 7.0 %collective-permute-start.22 = (f32[34,6,1,128]{3,0,2,1:T(8,128)S(1)}, f32[34,6,1,128]{3,0,2,1:T(8,128)S(1)}, u32[]{:S(2)}, u32[]{:S(2)}) collective-permute-start(f32[34,6,1,128]{3,0,2,1:T(8,128)S(1)} %copy.32), channel_id=1, source_target_pairs={{0,4},{1,5},{2,6},{3,7},{8,12},{9,13},{10,14},{11,15},{16,20},{17,... | collective-permute-start | bytes 313352 | tf_op jit(solution)/shard_map/ppermute | solution.py:17
where the time goes:
time: 247 us; the launch traced here: 246 us
  waiting for transfers between devices  122 us (49%)
  other arithmetic  64.9 us (26%)
  starting transfers between devices  49.2 us (20%)
  local copies, waits for them, and re-layouts  9.74 us (4%)
    ppermute x12, waiting for transfers between devices, padded_2(): lax.ppermute(tail, axis, [(i, (i + 1) % count) for i in range(ends)])  95.4 us
    add x4, other arithmetic, advance(): return middle + diffusivity * spread + source  62.3 us
    ppermute x12, starting transfers between devices, padded_2(): lax.ppermute(tail, axis, [(i, (i + 1) % count) for i in range(ends)])  33.7 us
    ppermute x12, waiting for transfers between devices, padded_2(): lax.ppermute(head, axis, [((i + 1) % count, i) for i in range(ends)])  26.6 us
    ppermute x12, starting transfers between devices, padded_2(): lax.ppermute(head, axis, [((i + 1) % count, i) for i in range(ends)])  15.5 us
  transfers between devices with their start and end apart: 24, of which 19 were waited for; matrix products, arithmetic and copies ran while one was open for 2% of the time, Pallas kernels for 0%

commit v1 on v0

v1 whole, which is shorter than its diff:
```python
import functools

import jax
import jax.numpy as jnp
from jax import lax
from jax.experimental import pallas as pl
from jax.experimental.pallas import tpu as pltpu
from jax.sharding import PartitionSpec as P

STEPS = 4
CHUNKS = 8
EDGE = 8
MESH = pl.DeviceIdType.MESH


def kernel(
    density,
    diffusivity,
    source,
    out,
    field,
    coef,
    src,
    result,
    k_out,
    k_in,
    load_sem,
    store_sem,
    i_send,
    i_recv,
    j_send,
    j_recv,
    k_send,
    k_recv,
):
    J, I, K, M = density.shape
    rows = J // CHUNKS
    cells = pl.ds(EDGE, K)

    def place(axis):
        me, count = lax.axis_index(axis), lax.axis_size(axis)
        return me, me > 0, me < count - 1

    pi, i_low, i_high = place("px")
    pj, j_low, j_high = place("py")
    pk, k_low, k_high = place("pz")
    has_low = {"px": i_low, "py": j_low, "pz": k_low}
    has_high = {"px": i_high, "py": j_high, "pz": k_high}
    me = {"px": pi, "py": pj, "pz": pk}

    def i_copy(side, step, chunk):
        at = pl.ds(chunk * rows, rows)
        padded = pl.ds(1 + chunk * rows, rows)
        if step == 0:
            face = density.at[at, (I - 1) if side == 0 else 0]
        else:
            face = field.at[step, padded, I if side == 0 else 1, cells]
        return pltpu.make_async_remote_copy(
            src_ref=face,
            dst_ref=field.at[step, padded, 0 if side == 0 else I + 1, cells],
            send_sem=i_send.at[side, step, chunk],
            recv_sem=i_recv.at[side, step, chunk],
            device_id={"px": pi + 1 if side == 0 else pi - 1},
            device_id_type=MESH,
        )

    def j_copy(side, step):
        if step == 0:
            face = density.at[(J - 1) if side == 0 else 0]
        else:
            face = field.at[step, J if side == 0 else 1, pl.ds(1, I), cells]
        return pltpu.make_async_remote_copy(
            src_ref=face,
            dst_ref=field.at[step, 0 if side == 0 else J + 1, pl.ds(1, I), cells],
            send_sem=j_send.at[side, step],
            recv_sem=j_recv.at[side, step],
            device_id={"py": pj + 1 if side == 0 else pj - 1},
            device_id_type=MESH,
        )

    def k_copy(side, step):
        return pltpu.make_async_remote_copy(
            src_ref=k_out.at[side, step],
            dst_ref=k_in.at[side, step],
            send_sem=k_send.at[side, step],
            recv_sem=k_recv.at[side, step],
            device_id={"pz": pk + 1 if side == 0 else pk - 1},
            device_id_type=MESH,
        )

    def goes(axis, side):
        return has_high[axis] if side == 0 else has_low[axis]

    def comes(axis, side):
        return has_low[axis] if side == 0 else has_high[axis]

    loads = [
        pltpu.make_async_copy(density, field.at[0, pl.ds(1, J), pl.ds(1, I), cells], load_sem.at[0]),
        pltpu.make_async_copy(diffusivity, coef, load_sem.at[1]),
        pltpu.make_async_copy(source, src, load_sem.at[2]),
    ]
    for load in loads:
        load.start()

    barrier = pltpu.get_barrier_semaphore()
    met = jnp.int32(0)
    for axis in ("px", "py", "pz"):
        for side in (0, 1):
            @pl.when(goes(axis, side))
            def _():
                pl.semaphore_signal(
                    barrier,
                    inc=1,
                    device_id={axis: me[axis] + 1 if side == 0 else me[axis] - 1},
                    device_id_type=MESH,
                )
            met = met + jnp.where(goes(axis, side), 1, 0).astype(jnp.int32)
    pl.semaphore_wait(barrier, met)

    for side in (0, 1):
        @pl.when(goes("px", side))
        def _():
            @pl.loop(0, CHUNKS)
            def _(chunk):
                i_copy(side, 0, chunk).start()

        @pl.when(goes("py", side))
        def _():
            j_copy(side, 0).start()

    for side in (0, 1):
        @pl.when(jnp.logical_not(comes("px", side)))
        def _():
            @pl.loop(0, J)
            def _(j):
                for step in range(STEPS):
                    field[step, j + 1, 0 if side == 0 else I + 1, cells, :] = jnp.zeros((K, M), jnp.float32)

        @pl.when(jnp.logical_not(comes("py", side)))
        def _():
            for step in range(STEPS):
                for i in range(I):
                    field[step, 0 if side == 0 else J + 1, i + 1, cells, :] = jnp.zeros((K, M), jnp.float32)

        @pl.when(jnp.logical_not(comes("pz", side)))
        def _():
            for step in range(STEPS):
                k_in[side, step] = jnp.zeros((J * I, M), jnp.float32)

    def pack(step, j):
        for i in range(I):
            at = pl.ds(j * I + i, 1)
            k_out[0, step, at, :] = field[step, j + 1, i + 1, pl.ds(EDGE + K - 1, 1), :]
            k_out[1, step, at, :] = field[step, j + 1, i + 1, pl.ds(EDGE, 1), :]

    loads[0].wait()

    @pl.loop(0, J)
    def _(j):
        pack(0, j)

    def start_k(step):
        for side in (0, 1):
            @pl.when(goes("pz", side))
            def _():
                k_copy(side, step).start()

    start_k(0)
    loads[1].wait()
    loads[2].wait()

    def stored(chunk):
        at = pl.ds(chunk * rows, rows)
        return pltpu.make_async_copy(result.at[at], out.at[at], store_sem.at[chunk])

    for step in range(STEPS):
        last = step == STEPS - 1
        for side in (0, 1):
            @pl.when(comes("py", side))
            def _():
                j_copy(side, step).wait_recv()

            @pl.when(comes("pz", side))
            def _():
                k_copy(side, step).wait_recv()

        @pl.loop(0, CHUNKS)
        def _(chunk):
            for side in (0, 1):
                @pl.when(comes("px", side))
                def _():
                    i_copy(side, step, chunk).wait_recv()

            @pl.loop(chunk * rows, (chunk + 1) * rows)
            def _(j):
                for i in range(I):
                    at = pl.ds(j * I + i, 1)
                    field[step, j + 1, i + 1, pl.ds(EDGE - 1, 1), :] = k_in[0, step, at, :]
                    field[step, j + 1, i + 1, pl.ds(EDGE + K, 1), :] = k_in[1, step, at, :]
                for i in range(I):
                    middle = field[step, j + 1, i + 1, cells, :]
                    spread = field[step, j, i + 1, cells, :] + field[step, j + 2, i + 1, cells, :]
                    spread = spread + field[step, j + 1, i, cells, :]
                    spread = spread + field[step, j + 1, i + 2, cells, :]
                    spread = spread + field[step, j + 1, i + 1, pl.ds(EDGE - 1, K), :]
                    spread = spread + field[step, j + 1, i + 1, pl.ds(EDGE + 1, K), :]
                    spread = spread - 6.0 * middle
                    value = middle + coef[j, i] * spread + src[j, i]
                    if last:
                        result[j, i] = value
                    else:
                        field[step + 1, j + 1, i + 1, cells, :] = value
                if not last:
                    pack(step + 1, j)

            if last:
                stored(chunk).start()
            else:
                for side in (0, 1):
                    @pl.when(goes("px", side))
                    def _():
                        i_copy(side, step + 1, chunk).start()

        if not last:
            for side in (0, 1):
                @pl.when(goes("py", side))
                def _():
                    j_copy(side, step + 1).start()
            start_k(step + 1)

    for side in (0, 1):
        @pl.when(goes("px", side))
        def _():
            for step in range(STEPS):
                @pl.loop(0, CHUNKS)
                def _(chunk):
                    i_copy(side, step, chunk).wait_send()

        @pl.when(goes("py", side))
        def _():
            for step in range(STEPS):
                j_copy(side, step).wait_send()

        @pl.when(goes("pz", side))
        def _():
            for step in range(STEPS):
                k_copy(side, step).wait_send()

    @pl.loop(0, CHUNKS)
    def _(chunk):
        stored(chunk).wait()


def body(density, diffusivity, source):
    J, I, K, M = density.shape
    f32 = jnp.float32
    any_space = pl.BlockSpec(memory_space=pl.ANY)
    dma = pltpu.SemaphoreType.DMA
    return pl.pallas_call(
        kernel,
        out_shape=jax.ShapeDtypeStruct((J, I, K, M), f32),
        in_specs=[any_space] * 3,
        out_specs=any_space,
        scratch_shapes=[
            pltpu.VMEM((STEPS, J + 2, I + 2, K + 2 * EDGE, M), f32),
            pltpu.VMEM((J, I, K, M), f32),
            pltpu.VMEM((J, I, K, M), f32),
            pltpu.VMEM((J, I, K, M), f32),
            pltpu.VMEM((2, STEPS, J * I, M), f32),
            pltpu.VMEM((2, STEPS, J * I, M), f32),
            dma((3,)),
            dma((CHUNKS,)),
            dma((2, STEPS, CHUNKS)),
            dma((2, STEPS, CHUNKS)),
            dma((2, STEPS)),
            dma((2, STEPS)),
            dma((2, STEPS)),
            dma((2, STEPS)),
        ],
        compiler_params=pltpu.CompilerParams(
            collective_id=0, has_side_effects=True, vmem_limit_bytes=60 * 1024 * 1024
        ),
    )(density, diffusivity, source)


def solution(mesh):
    placed = P(("site", "py"), "px", "pz", None)
    return jax.shard_map(body, mesh=mesh, in_specs=(placed,) * 3, out_specs=placed, check_vma=False)
```

time: 247 us -> 102 us (0.41)
  waiting for transfers between devices: 122 us -> 0 us
  Pallas kernels: 0 us -> 97.5 us
  other arithmetic: 64.9 us -> 0 us
  starting transfers between devices: 49.2 us -> 0 us
  local copies, waits for them, and re-layouts: 9.74 us -> 4.79 us
    ppermute x24 -> x0, waiting for transfers between devices: 122 us -> none  [the longest x12 95.4 us: padded_2(): lax.ppermute(tail, axis, [(i, (i + 1) % count) for i in range(ends)])]
    pallas_call x0 -> x1, Pallas kernels: none -> 97.5 us  [body(): pl.pallas_call(kernel, out_shape=jax.ShapeDtypeStruct((J, I, K, M), f32),...]
    add x4 -> x0, other arithmetic: 62.3 us -> none  [advance(): return middle + diffusivity * spread + source]
    ppermute x24 -> x0, starting transfers between devices: 49.2 us -> none  [the longest x12 33.7 us: padded_2(): lax.ppermute(tail, axis, [(i, (i + 1) % count) for i in range(ends)])]
    ppermute x8 -> x0, local copies, waits for them, and re-layouts: 4.7 us -> none  [the longest x4 2.35 us: padded_2(): lax.ppermute(head, axis, [((i + 1) % count, i) for i in range(ends)])]
    slice x7 -> x0, other arithmetic: 2.68 us -> none  [padded_2(): lax.slice_in_dim(cells, cells.shape[dim] - width, cells.shape[dim], axis=...]
    slice x13 -> x0, local copies, waits for them, and re-layouts: 2.5 us -> none  [the longest x8 1.47 us: padded_2(): lax.slice_in_dim(cells, cells.shape[dim] - width, cells.shape[dim], axis=...]
  transfers between devices with their start and end apart: 24 -> 0, of which waited for: 19 -> 0; matrix products, arithmetic and copies ran while one was open for 2% -> 0% of each run, Pallas kernels for 0% -> 0%
where the time goes in v1:
time: 102 us
  Pallas kernels  97.5 us (96%)
  local copies, waits for them, and re-layouts  4.79 us (5%)
    pallas_call x1, Pallas kernels, body(): pl.pallas_call(kernel, out_shape=jax.ShapeDtypeStruct((J, I, K, M), f32),...  97.5 us
    unnamed x1, local copies, waits for them, and re-layouts  4.79 us

profile of v1, /device:TPU:0, one launch (start us, length us, event | category | flops | bytes accessed | tf_op | source)
XLA Modules:
  0.0 102.3 jit_solution(11627987389610834469)
XLA Ops:
  0.0 97.5 %shard_map.37 = f32[32,4,64,128]{3,2,1,0:T(8,128)} custom-call(f32[32,4,64,128]{3,2,1,0:T(8,128)} %density.1, f32[32,4,64,128]{3,2,1,0:T(8,128)} %diffusivity.1, f32[32,4,64,128]{3,2,1,0:T(8,128)} %source.1), custom_call_target="tpu_custom_call" | custom-call | tf_op jit(solution)/shard_map/pallas_call | solution.py:259
  97.5 4.8 %copy.5 = f32[32,4,64,128]{3,2,1,0:T(8,128)} copy(f32[32,4,64,128]{3,2,1,0:T(8,128)} %shard_map.37) | data formatting | bytes 8388608

commit v2 on v1

--- a/solution.py
+++ b/solution.py
@@ -8,24 +8,43 @@
 from jax.sharding import PartitionSpec as P
 
 STEPS = 4
-CHUNKS = 8
+CHUNKS = 4
+SHORTEST = 2
 EDGE = 8
 MESH = pl.DeviceIdType.MESH
+
+
+def chunks_of(J, step):
+    if step < STEPS - 1:
+        rows = J // CHUNKS
+        return [(start, rows) for start in range(0, J, rows)]
+    found, start, rows = [], 0, J // 2
+    while start < J:
+        found.append((start, rows))
+        start += rows
+        rows = max(min(rows // 2, J - start), min(SHORTEST, J - start))
+    return found
+
+
+def segments_of(J, step):
+    cuts = {start for start, _ in chunks_of(J, step)} | {J}
+    if step < STEPS - 1:
+        cuts |= {start for start, _ in chunks_of(J, step + 1)}
+    cuts = sorted(cuts)
+    return list(zip(cuts[:-1], cuts[1:]))
 
 
 def kernel(
     density,
     diffusivity,
     source,
-    out,
+    result,
     field,
     coef,
     src,
-    result,
     k_out,
     k_in,
     load_sem,
-    store_sem,
     i_send,
     i_recv,
     j_send,
@@ -34,7 +53,6 @@
     k_recv,
 ):
     J, I, K, M = density.shape
-    rows = J // CHUNKS
     cells = pl.ds(EDGE, K)
 
     def place(axis):
@@ -49,14 +67,10 @@
     me = {"px": pi, "py": pj, "pz": pk}
 
     def i_copy(side, step, chunk):
-        at = pl.ds(chunk * rows, rows)
-        padded = pl.ds(1 + chunk * rows, rows)
-        if step == 0:
-            face = density.at[at, (I - 1) if side == 0 else 0]
-        else:
-            face = field.at[step, padded, I if side == 0 else 1, cells]
+        start, rows = chunks_of(J, step)[chunk]
+        padded = pl.ds(1 + start, rows)
         return pltpu.make_async_remote_copy(
-            src_ref=face,
+            src_ref=field.at[step, padded, I if side == 0 else 1, cells],
             dst_ref=field.at[step, padded, 0 if side == 0 else I + 1, cells],
             send_sem=i_send.at[side, step, chunk],
             recv_sem=i_recv.at[side, step, chunk],
@@ -94,13 +108,21 @@
     def comes(axis, side):
         return has_low[axis] if side == 0 else has_high[axis]
 
+    def load(chunk):
+        start, rows = chunks_of(J, 0)[chunk]
+        return pltpu.make_async_copy(
+            density.at[pl.ds(start, rows)],
+            field.at[0, pl.ds(1 + start, rows), pl.ds(1, I), cells],
+            load_sem.at[2 + chunk],
+        )
+
+    first = range(len(chunks_of(J, 0)))
     loads = [
-        pltpu.make_async_copy(density, field.at[0, pl.ds(1, J), pl.ds(1, I), cells], load_sem.at[0]),
-        pltpu.make_async_copy(diffusivity, coef, load_sem.at[1]),
-        pltpu.make_async_copy(source, src, load_sem.at[2]),
+        pltpu.make_async_copy(diffusivity, coef, load_sem.at[0]),
+        pltpu.make_async_copy(source, src, load_sem.at[1]),
     ]
-    for load in loads:
-        load.start()
+    for chunk in first:
+        load(chunk).start()
 
     barrier = pltpu.get_barrier_semaphore()
     met = jnp.int32(0)
@@ -117,16 +139,20 @@
             met = met + jnp.where(goes(axis, side), 1, 0).astype(jnp.int32)
     pl.semaphore_wait(barrier, met)
 
+    for chunk in first:
+        load(chunk).wait()
+        for side in (0, 1):
+            @pl.when(goes("px", side))
+            def _():
+                i_copy(side, 0, chunk).start()
+
     for side in (0, 1):
-        @pl.when(goes("px", side))
-        def _():
-            @pl.loop(0, CHUNKS)
-            def _(chunk):
-                i_copy(side, 0, chunk).start()
-
         @pl.when(goes("py", side))
         def _():
             j_copy(side, 0).start()
+
+    for one in loads:
+        one.start()
 
     for side in (0, 1):
         @pl.when(jnp.logical_not(comes("px", side)))
@@ -153,8 +179,6 @@
             k_out[0, step, at, :] = field[step, j + 1, i + 1, pl.ds(EDGE + K - 1, 1), :]
             k_out[1, step, at, :] = field[step, j + 1, i + 1, pl.ds(EDGE, 1), :]
 
-    loads[0].wait()
-
     @pl.loop(0, J)
     def _(j):
         pack(0, j)
@@ -166,12 +190,8 @@
                 k_copy(side, step).start()
 
     start_k(0)
-    loads[1].wait()
-    loads[2].wait()
-
-    def stored(chunk):
-        at = pl.ds(chunk * rows, rows)
-        return pltpu.make_async_copy(result.at[at], out.at[at], store_sem.at[chunk])
+    for one in loads:
+        one.wait()
 
     for step in range(STEPS):
         last = step == STEPS - 1
@@ -184,14 +204,15 @@
             def _():
                 k_copy(side, step).wait_recv()
 
-        @pl.loop(0, CHUNKS)
-        def _(chunk):
-            for side in (0, 1):
-                @pl.when(comes("px", side))
-                def _():
-                    i_copy(side, step, chunk).wait_recv()
-
-            @pl.loop(chunk * rows, (chunk + 1) * rows)
+        for begin, end in segments_of(J, step):
+            for chunk, (start, _) in enumerate(chunks_of(J, step)):
+                if start == begin:
+                    for side in (0, 1):
+                        @pl.when(comes("px", side))
+                        def _():
+                            i_copy(side, step, chunk).wait_recv()
+
+            @pl.loop(begin, end)
             def _(j):
                 for i in range(I):
                     at = pl.ds(j * I + i, 1)
@@ -213,13 +234,13 @@
                 if not last:
                     pack(step + 1, j)
 
-            if last:
-                stored(chunk).start()
-            else:
-                for side in (0, 1):
-                    @pl.when(goes("px", side))
-                    def _():
-                        i_copy(side, step + 1, chunk).start()
+            if not last:
+                for chunk, (start, rows) in enumerate(chunks_of(J, step + 1)):
+                    if start + rows == end:
+                        for side in (0, 1):
+                            @pl.when(goes("px", side))
+                            def _():
+                                i_copy(side, step + 1, chunk).start()
 
         if not last:
             for side in (0, 1):
@@ -232,8 +253,7 @@
         @pl.when(goes("px", side))
         def _():
             for step in range(STEPS):
-                @pl.loop(0, CHUNKS)
-                def _(chunk):
+                for chunk in range(len(chunks_of(J, step))):
                     i_copy(side, step, chunk).wait_send()
 
         @pl.when(goes("py", side))
@@ -246,41 +266,56 @@
             for step in range(STEPS):
                 k_copy(side, step).wait_send()
 
-    @pl.loop(0, CHUNKS)
-    def _(chunk):
-        stored(chunk).wait()
+
+def store_kernel(result, out, sem):
+    rows = result.shape[0] // CHUNKS
+    copies = [
+        pltpu.make_async_copy(result.at[pl.ds(c * rows, rows)], out.at[pl.ds(c * rows, rows)], sem.at[c])
+        for c in range(CHUNKS)
+    ]
+    for copy in copies:
+        copy.start()
+    for copy in copies:
+        copy.wait()
 
 
 def body(density, diffusivity, source):
     J, I, K, M = density.shape
     f32 = jnp.float32
+    copies = max(len(chunks_of(J, step)) for step in range(STEPS))
     any_space = pl.BlockSpec(memory_space=pl.ANY)
     dma = pltpu.SemaphoreType.DMA
-    return pl.pallas_call(
+    result = pl.pallas_call(
         kernel,
-        out_shape=jax.ShapeDtypeStruct((J, I, K, M), f32),
+        out_shape=pltpu.VMEM((J, I, K, M), f32),
         in_specs=[any_space] * 3,
-        out_specs=any_space,
+        out_specs=pl.BlockSpec(memory_space=pltpu.VMEM),
         scratch_shapes=[
             pltpu.VMEM((STEPS, J + 2, I + 2, K + 2 * EDGE, M), f32),
             pltpu.VMEM((J, I, K, M), f32),
             pltpu.VMEM((J, I, K, M), f32),
-            pltpu.VMEM((J, I, K, M), f32),
             pltpu.VMEM((2, STEPS, J * I, M), f32),
             pltpu.VMEM((2, STEPS, J * I, M), f32),
-            dma((3,)),
-            dma((CHUNKS,)),
-            dma((2, STEPS, CHUNKS)),
-            dma((2, STEPS, CHUNKS)),
+            dma((2 + CHUNKS,)),
+            dma((2, STEPS, copies)),
+            dma((2, STEPS, copies)),
             dma((2, STEPS)),
             dma((2, STEPS)),
             dma((2, STEPS)),
             dma((2, STEPS)),
         ],
         compiler_params=pltpu.CompilerParams(
-            collective_id=0, has_side_effects=True, vmem_limit_bytes=60 * 1024 * 1024
+            collective_id=0, has_side_effects=True, vmem_limit_bytes=46 * 1024 * 1024
         ),
     )(density, diffusivity, source)
+    return pl.pallas_call(
+        store_kernel,
+        out_shape=jax.ShapeDtypeStruct((J, I, K, M), f32),
+        in_specs=[pl.BlockSpec(memory_space=pltpu.VMEM)],
+        out_specs=any_space,
+        scratch_shapes=[dma((CHUNKS,))],
+        compiler_params=pltpu.CompilerParams(vmem_limit_bytes=1024 * 1024),
+    )(result)
 
 
 def solution(mesh):

time: 102 us -> 98.2 us (0.963)
  local copies, waits for them, and re-layouts: 4.79 us -> 0 us
    unnamed x1 -> x0, local copies, waits for them, and re-layouts: 4.79 us -> none
    pallas_call x1 -> x2, Pallas kernels: 97.5 us -> 98 us  [the longest x1 96 us: body(): pl.pallas_call(kernel, out_shape=pltpu.VMEM((J, I, K, M), f32), in_specs=...]
where the time goes in v2:
time: 98.2 us; the launch traced here: 98 us
  Pallas kernels  98 us (100%)
    pallas_call x1, Pallas kernels, body(): pl.pallas_call(kernel, out_shape=pltpu.VMEM((J, I, K, M), f32), in_specs=...  96 us
    pallas_call x1, Pallas kernels, body(): pl.pallas_call(store_kernel, out_shape=jax.ShapeDtypeStruct((J, I, K, M),...  2.04 us

profile of v2, /device:TPU:0, one launch (start us, length us, event | category | flops | bytes accessed | tf_op | source)
XLA Modules:
  0.0 98.0 jit_solution(6336704036745173462)
XLA Ops:
  0.0 96.0 %shard_map.37.result = f32[32,4,64,128]{3,2,1,0:T(8,128)S(1)} custom-call(f32[32,4,64,128]{3,2,1,0:T(8,128)} %density.1, f32[32,4,64,128]{3,2,1,0:T(8,128)} %diffusivity.1, f32[32,4,64,128]{3,2,1,0:T(8,128)} %source.1), custom_call_target="tpu_custom_call" | custom-call | tf_op jit(solution)/shard_map/pallas_call | solution.py:288
  96.0 2.0 %shard_map.38 = f32[32,4,64,128]{3,2,1,0:T(8,128)} custom-call(f32[32,4,64,128]{3,2,1,0:T(8,128)S(1)} %shard_map.37.result), custom_call_target="tpu_custom_call" | custom-call | tf_op jit(solution)/shard_map/pallas_call | solution.py:311

commit v3 on v2

--- a/solution.py
+++ b/solution.py
@@ -108,21 +108,21 @@
     def comes(axis, side):
         return has_low[axis] if side == 0 else has_high[axis]
 
-    def load(chunk):
+    def load(chunk, planes, count, sem):
         start, rows = chunks_of(J, 0)[chunk]
         return pltpu.make_async_copy(
-            density.at[pl.ds(start, rows)],
-            field.at[0, pl.ds(1 + start, rows), pl.ds(1, I), cells],
-            load_sem.at[2 + chunk],
+            density.at[pl.ds(start, rows), pl.ds(planes, count)],
+            field.at[0, pl.ds(1 + start, rows), pl.ds(1 + planes, count), cells],
+            load_sem.at[sem],
         )
 
-    first = range(len(chunks_of(J, 0)))
+    faces = [load(0, 0, 1, 0), load(0, I - 1, 1, 1)]
+    inner = load(0, 1, I - 2, 2)
+    others = [load(chunk, 0, I, 2 + chunk) for chunk in range(1, len(chunks_of(J, 0)))]
     loads = [
-        pltpu.make_async_copy(diffusivity, coef, load_sem.at[0]),
-        pltpu.make_async_copy(source, src, load_sem.at[1]),
+        pltpu.make_async_copy(diffusivity, coef, load_sem.at[2 + CHUNKS]),
+        pltpu.make_async_copy(source, src, load_sem.at[3 + CHUNKS]),
     ]
-    for chunk in first:
-        load(chunk).start()
 
     barrier = pltpu.get_barrier_semaphore()
     met = jnp.int32(0)
@@ -137,14 +137,25 @@
                     device_id_type=MESH,
                 )
             met = met + jnp.where(goes(axis, side), 1, 0).astype(jnp.int32)
+    for one in faces:
+        one.start()
     pl.semaphore_wait(barrier, met)
 
-    for chunk in first:
-        load(chunk).wait()
+    def start_i(chunk):
         for side in (0, 1):
             @pl.when(goes("px", side))
             def _():
                 i_copy(side, 0, chunk).start()
+
+    for one in faces:
+        one.wait()
+    start_i(0)
+    for one in (*others, inner):
+        one.start()
+    for chunk, one in enumerate(others, 1):
+        one.wait()
+        start_i(chunk)
+    inner.wait()
 
     for side in (0, 1):
         @pl.when(goes("py", side))
@@ -296,7 +307,7 @@
             pltpu.VMEM((J, I, K, M), f32),
             pltpu.VMEM((2, STEPS, J * I, M), f32),
             pltpu.VMEM((2, STEPS, J * I, M), f32),
-            dma((2 + CHUNKS,)),
+            dma((4 + CHUNKS,)),
             dma((2, STEPS, copies)),
             dma((2, STEPS, copies)),
             dma((2, STEPS)),

time: 98.2 us -> 98.2 us (level)
  no operation moved by 1% of the time
where the time goes in v3:
time: 98.2 us; the launch traced here: 98.1 us
  Pallas kernels  98 us (100%)
    pallas_call x1, Pallas kernels, body(): pl.pallas_call(kernel, out_shape=pltpu.VMEM((J, I, K, M), f32), in_specs=...  96 us
    pallas_call x1, Pallas kernels, body(): pl.pallas_call(store_kernel, out_shape=jax.ShapeDtypeStruct((J, I, K, M),...  2.04 us

profile of v3, /device:TPU:0, one launch (start us, length us, event | category | flops | bytes accessed | tf_op | source)
XLA Modules:
  0.0 98.1 jit_solution(5781387024356365187)
XLA Ops:
  0.0 96.0 %shard_map.37.result = f32[32,4,64,128]{3,2,1,0:T(8,128)S(1)} custom-call(f32[32,4,64,128]{3,2,1,0:T(8,128)} %density.1, f32[32,4,64,128]{3,2,1,0:T(8,128)} %diffusivity.1, f32[32,4,64,128]{3,2,1,0:T(8,128)} %source.1), custom_call_target="tpu_custom_call" | custom-call | tf_op jit(solution)/shard_map/pallas_call | solution.py:299
  96.0 2.0 %shard_map.38 = f32[32,4,64,128]{3,2,1,0:T(8,128)} custom-call(f32[32,4,64,128]{3,2,1,0:T(8,128)S(1)} %shard_map.37.result), custom_call_target="tpu_custom_call" | custom-call | tf_op jit(solution)/shard_map/pallas_call | solution.py:322
